TPU v7x, 256 devices: a whole 4x4x8 slice. The times are simulated.
256 devices in a mesh: outer: 16 (over z_lo, y), inner: 16 (over x, z_hi, core).
Axes of the slice: x: 4, y: 4, z: 8 (z_hi: 2, z_lo: 4; z = z_hi * 4 + z_lo), core: 2. Of those that a mesh axis runs over, the one named last changes fastest.
Arguments:
- stem_real: float32 [16, 16, 256, 512], P('outer', 'inner'), may hold values from -6 to 6
- stem_imag: float32 [16, 16, 256, 512], P('outer', 'inner'), may hold values from -6 to 6
- branch_real: float32 [4, 512, 512], replicated, may hold values from -0.1875 to 0.1875
- branch_imag: float32 [4, 512, 512], replicated, may hold values from -0.1875 to 0.1875
- orders: int32 [4, 512], replicated, may hold values from 0 to 511, each once within a row
Outputs:
- out_real: float32 [16, 16, 256, 512], P('outer', 'inner')
- out_imag: float32 [16, 16, 256, 512], P('outer', 'inner')
Inputs may be any that keep to these rules, and one draw needn't show every extreme that they name: Each row of orders holds every index of 0 to 511 once.
All inputs are finite; a program needn't handle non-finite values.
Results may differ from a plain program's by a relative error of at most 0.0001.
Values sent between devices are 32-bit elements; how exact they have to be, the bound alone decides.
No kernel may reach another device: no remote copies, remote signals or barrier semaphores. Data moves between devices by JAX's collectives and lax.ppermute only.
A program may use at most 64 MiB of HBM per device.

v0:
```python
import jax
import jax.numpy as jnp
from jax import lax
from jax.sharding import PartitionSpec as P

PRODUCTS = 4


def prepare(branch_real, branch_imag, order):
    width = branch_real.shape[0]
    places = lax.broadcasted_iota(jnp.int32, (width, width), 0)
    selector = (places == order[None, :]).astype(jnp.float32)
    moved_real = jnp.dot(
        selector, branch_real, precision=lax.Precision.HIGHEST, preferred_element_type=jnp.float32
    )
    moved_imag = jnp.dot(
        selector, branch_imag, precision=lax.Precision.HIGHEST, preferred_element_type=jnp.float32
    )
    return (moved_real, moved_imag, moved_real + moved_imag)


def product(plane_real, plane_imag, prepared):
    moved_real, moved_imag, moved_sum = prepared
    width = moved_real.shape[0]
    count = plane_real.size // width
    left_real = plane_real.reshape(count, width)
    left_imag = plane_imag.reshape(count, width)
    first = jnp.dot(
        left_real, moved_real, precision=lax.Precision.HIGHEST, preferred_element_type=jnp.float32
    )
    second = jnp.dot(
        left_imag, moved_imag, precision=lax.Precision.HIGHEST, preferred_element_type=jnp.float32
    )
    third = jnp.dot(
        left_real + left_imag,
        moved_sum,
        precision=lax.Precision.HIGHEST,
        preferred_element_type=jnp.float32,
    )
    return (
        (first - second).reshape(1, 1, count, width),
        (third - first - second).reshape(1, 1, count, width),
    )


def inner_step(plane_real, plane_imag, prepared):
    return product(
        lax.all_to_all(plane_real, "inner", split_axis=3, concat_axis=3, tiled=True),
        lax.all_to_all(plane_imag, "inner", split_axis=3, concat_axis=3, tiled=True),
        prepared,
    )


def outer_step(plane_real, plane_imag, prepared):
    return product(
        lax.all_to_all(plane_real, "outer", split_axis=3, concat_axis=3, tiled=True),
        lax.all_to_all(plane_imag, "outer", split_axis=3, concat_axis=3, tiled=True),
        prepared,
    )


def on_device(stem_real, stem_imag, branch_real, branch_imag, orders):
    tables = [
        prepare(branch_real[step], branch_imag[step], orders[step]) for step in range(PRODUCTS)
    ]
    plane_real, plane_imag = product(stem_real, stem_imag, tables[0])
    plane_real, plane_imag = inner_step(plane_real, plane_imag, tables[1])
    plane_real, plane_imag = outer_step(plane_real, plane_imag, tables[2])
    plane_real, plane_imag = inner_step(plane_real, plane_imag, tables[3])
    return (plane_real, plane_imag)


def solution(mesh):
    placed = (P("outer", "inner", None, None), P("outer", "inner", None, None), P(), P(), P())
    return jax.shard_map(
        on_device,
        mesh=mesh,
        in_specs=placed,
        out_specs=(P("outer", "inner", None, None), P("outer", "inner", None, None)),
        check_vma=False,
    )
```

profile of v0, /device:TPU:33, one launch (start us, length us, event | category | flops | bytes accessed | tf_op | source)
XLA Modules:
  0.0 170.0 jit_solution(8441266659975682407)
XLA Ops:
  1.5 2.3 %fusion.20 = f32[512,512]{1,0:T(8,128)S(1)} fusion(f32[4,512,512]{2,1,0:T(8,128)} %param.8, s32[512]{0:T(512)S(1)} %bitcast.110), kind=kOutput, calls=%fused_computation.26 | convolution fusion | flops 1610874880 | bytes 2099200 | tf_op jit(solution)/shard_map/dot_general | solution.py:16
  3.8 2.3 %fusion.22 = f32[512,512]{1,0:T(8,128)S(1)} fusion(f32[4,512,512]{2,1,0:T(8,128)} %param.7, s32[512]{0:T(512)S(1)} %bitcast.111), kind=kOutput, calls=%fused_computation.28 | convolution fusion | flops 1610874880 | bytes 2099200 | tf_op jit(solution)/shard_map/dot_general | solution.py:13
  13.0 10.7 %all-to-all-start.1 = ((f32[1,1,256,512]{2,1,0,3:T(1,128)}), f32[1,1,256,512]{2,1,0,3:T(1,128)S(1)}, u32[]{:S(2)}, u32[]{:S(2)}) async-start(f32[1,1,256,512]{2,1,0,3:T(1,128)} %copy.10), calls=%async_computation.1 | async-start | bytes 1048576 | tf_op jit(solution)/shard_map/all_to_all | solution.py:49
  25.1 17.8 %all-to-all-done.1 = f32[1,1,256,512]{2,1,0,3:T(1,128)S(1)} async-done(((f32[1,1,256,512]{2,1,0,3:T(1,128)}), f32[1,1,256,512]{2,1,0,3:T(1,128)S(1)}, u32[]{:S(2)}, u32[]{:S(2)}) %all-to-all-start.1) | async-done | bytes 524320 | tf_op jit(solution)/shard_map/all_to_all | solution.py:49
  42.9 5.2 %all-to-all-start = ((f32[1,1,256,512]{2,1,0,3:T(1,128)}), f32[1,1,256,512]{2,1,0,3:T(1,128)}, u32[]{:S(2)}, u32[]{:S(2)}) async-start(f32[1,1,256,512]{2,1,0,3:T(1,128)} %copy.8), calls=%async_computation | async-start | bytes 1048576 | tf_op jit(solution)/shard_map/all_to_all | solution.py:48
  48.1 2.3 %fusion.16 = f32[512,512]{1,0:T(8,128)S(1)} fusion(f32[4,512,512]{2,1,0:T(8,128)} %param.8, s32[512]{0:T(512)S(1)} %bitcast.108), kind=kOutput, calls=%fused_computation.22 | convolution fusion | flops 1610874880 | bytes 2099200 | tf_op jit(solution)/shard_map/dot_general | solution.py:16
  50.4 2.3 %fusion.18 = f32[512,512]{1,0:T(8,128)S(1)} fusion(f32[4,512,512]{2,1,0:T(8,128)} %param.7, s32[512]{0:T(512)S(1)} %bitcast.109), kind=kOutput, calls=%fused_computation.24 | convolution fusion | flops 1610874880 | bytes 2099200 | tf_op jit(solution)/shard_map/dot_general | solution.py:13
  53.8 11.0 %all-to-all-done = f32[1,1,256,512]{2,1,0,3:T(1,128)} async-done(((f32[1,1,256,512]{2,1,0,3:T(1,128)}), f32[1,1,256,512]{2,1,0,3:T(1,128)}, u32[]{:S(2)}, u32[]{:S(2)}) %all-to-all-start) | async-done | bytes 524320 | tf_op jit(solution)/shard_map/all_to_all | solution.py:48
  66.9 3.1 %fusion.3 = f32[1,1,256,512]{3,2,1,0:T(8,128)} fusion(f32[256,512]{1,0:T(8,128)S(1)} %fusion.46, f32[256,512]{1,0:T(8,128)S(1)} %fusion.49, f32[512,512]{1,0:T(8,128)S(1)} %fusion.18, f32[512,512]{1,0:T(8,128)S(1)} %fusion.16, f32[1,1,256,512]{2,1,0,3:T(1,128)} %copy-done.2, f32[1,1,256,512]{2,1,0,3:T(1,128)} %all-to-all-done), kind=kOutput, calls=%fused_computation.7 | convolution fusion | flops 805961728 | bytes 4718592 | tf_op jit(solution)/shard_map/dot_general | solution.py:34
  72.0 5.8 %all-to-all-start.3 = ((f32[1,1,256,512]{2,1,0,3:T(1,128)}), f32[1,1,256,512]{2,1,0,3:T(1,128)S(1)}, u32[]{:S(2)}, u32[]{:S(2)}) async-start(f32[1,1,256,512]{2,1,0,3:T(1,128)} %copy.12), calls=%async_computation.3 | async-start | bytes 1048576 | tf_op jit(solution)/shard_map/all_to_all | solution.py:57
  78.9 12.9 %all-to-all-done.3 = f32[1,1,256,512]{2,1,0,3:T(1,128)S(1)} async-done(((f32[1,1,256,512]{2,1,0,3:T(1,128)}), f32[1,1,256,512]{2,1,0,3:T(1,128)S(1)}, u32[]{:S(2)}, u32[]{:S(2)}) %all-to-all-start.3) | async-done | bytes 524320 | tf_op jit(solution)/shard_map/all_to_all | solution.py:57
  91.8 5.1 %all-to-all-start.2 = ((f32[1,1,256,512]{2,1,0,3:T(1,128)}), f32[1,1,256,512]{2,1,0,3:T(1,128)}, u32[]{:S(2)}, u32[]{:S(2)}) async-start(f32[1,1,256,512]{2,1,0,3:T(1,128)} %copy.11), calls=%async_computation.2 | async-start | bytes 1048576 | tf_op jit(solution)/shard_map/all_to_all | solution.py:56
  96.9 2.4 %fusion.12 = f32[512,512]{1,0:T(8,128)S(1)} fusion(f32[4,512,512]{2,1,0:T(8,128)} %param.8, s32[512]{0:T(512)S(1)} %bitcast.106), kind=kOutput, calls=%fused_computation.18 | convolution fusion | flops 1610874880 | bytes 2099200 | tf_op jit(solution)/shard_map/dot_general | solution.py:16
  99.3 2.3 %fusion.14 = f32[512,512]{1,0:T(8,128)S(1)} fusion(f32[4,512,512]{2,1,0:T(8,128)} %param.7, s32[512]{0:T(512)S(1)} %bitcast.107), kind=kOutput, calls=%fused_computation.20 | convolution fusion | flops 1610874880 | bytes 2099200 | tf_op jit(solution)/shard_map/dot_general | solution.py:13
  102.7 7.9 %all-to-all-done.2 = f32[1,1,256,512]{2,1,0,3:T(1,128)} async-done(((f32[1,1,256,512]{2,1,0,3:T(1,128)}), f32[1,1,256,512]{2,1,0,3:T(1,128)}, u32[]{:S(2)}, u32[]{:S(2)}) %all-to-all-start.2) | async-done | bytes 524320 | tf_op jit(solution)/shard_map/all_to_all | solution.py:56
  110.6 2.1 %fusion.44 = f32[256,512]{1,0:T(8,128)S(1)} fusion(f32[512,512]{1,0:T(8,128)S(1)} %fusion.14, f32[1,1,256,512]{2,1,0,3:T(1,128)} %all-to-all-done.2), kind=kOutput, calls=%fused_computation.56 | convolution fusion | flops 805306368 | bytes 2097152 | tf_op jit(solution)/shard_map/dot_general | solution.py:28
  112.7 3.1 %fusion.5 = f32[1,1,256,512]{3,2,1,0:T(8,128)} fusion(f32[256,512]{1,0:T(8,128)S(1)} %fusion.41, f32[256,512]{1,0:T(8,128)S(1)} %fusion.44, f32[512,512]{1,0:T(8,128)S(1)} %fusion.14, f32[512,512]{1,0:T(8,128)S(1)} %fusion.12, f32[1,1,256,512]{2,1,0,3:T(1,128)} %copy-done.3, f32[1,1,256,512]{2,1,0,3:T(1,128)} %all-to-all-done.2), kind=kOutput, calls=%fused_computation.9 | convolution fusion | flops 805961728 | bytes 4718592 | tf_op jit(solution)/shard_map/dot_general | solution.py:34
  117.8 5.8 %all-to-all-start.5 = ((f32[1,1,256,512]{2,1,0,3:T(1,128)}), f32[1,1,256,512]{2,1,0,3:T(1,128)S(1)}, u32[]{:S(2)}, u32[]{:S(2)}) async-start(f32[1,1,256,512]{2,1,0,3:T(1,128)} %copy.14), calls=%async_computation.5 | async-start | bytes 1048576 | tf_op jit(solution)/shard_map/all_to_all | solution.py:49
  124.7 18.2 %all-to-all-done.5 = f32[1,1,256,512]{2,1,0,3:T(1,128)S(1)} async-done(((f32[1,1,256,512]{2,1,0,3:T(1,128)}), f32[1,1,256,512]{2,1,0,3:T(1,128)S(1)}, u32[]{:S(2)}, u32[]{:S(2)}) %all-to-all-start.5) | async-done | bytes 524320 | tf_op jit(solution)/shard_map/all_to_all | solution.py:49
  142.9 5.2 %all-to-all-start.4 = ((f32[1,1,256,512]{2,1,0,3:T(1,128)}), f32[1,1,256,512]{2,1,0,3:T(1,128)}, u32[]{:S(2)}, u32[]{:S(2)}) async-start(f32[1,1,256,512]{2,1,0,3:T(1,128)} %copy.13), calls=%async_computation.4 | async-start | bytes 1048576 | tf_op jit(solution)/shard_map/all_to_all | solution.py:48
  148.1 2.4 %fusion.8 = f32[512,512]{1,0:T(8,128)S(1)} fusion(f32[4,512,512]{2,1,0:T(8,128)} %param.8, s32[512]{0:T(512)S(1)} %bitcast.104), kind=kOutput, calls=%fused_computation.14 | convolution fusion | flops 1610874880 | bytes 2099200 | tf_op jit(solution)/shard_map/dot_general | solution.py:16
  150.5 2.3 %fusion.10 = f32[512,512]{1,0:T(8,128)S(1)} fusion(f32[4,512,512]{2,1,0:T(8,128)} %param.7, s32[512]{0:T(512)S(1)} %bitcast.105), kind=kOutput, calls=%fused_computation.16 | convolution fusion | flops 1610874880 | bytes 2099200 | tf_op jit(solution)/shard_map/dot_general | solution.py:13
  153.9 10.2 %all-to-all-done.4 = f32[1,1,256,512]{2,1,0,3:T(1,128)} async-done(((f32[1,1,256,512]{2,1,0,3:T(1,128)}), f32[1,1,256,512]{2,1,0,3:T(1,128)}, u32[]{:S(2)}, u32[]{:S(2)}) %all-to-all-start.4) | async-done | bytes 524320 | tf_op jit(solution)/shard_map/all_to_all | solution.py:48
  167.1 3.0 %fusion.7 = f32[1,1,256,512]{3,2,1,0:T(8,128)} fusion(f32[256,512]{1,0:T(8,128)S(1)} %fusion.36, f32[256,512]{1,0:T(8,128)S(1)} %fusion.39, f32[512,512]{1,0:T(8,128)S(1)} %fusion.10, f32[512,512]{1,0:T(8,128)S(1)} %fusion.8, f32[1,1,256,512]{2,1,0,3:T(1,128)S(1)} %copy-done.1, f32[1,1,256,512]{2,1,0,3:T(1,128)} %all-to-all-done.4), kind=kOutput, calls=%fused_computation.11 | convolution fusion | flops 805961728 | bytes 4718592 | tf_op jit(solution)/shard_map/dot_general | solution.py:34
  (33 shorter events, 23.4 us)
Async XLA Ops:
  0.6 5.5 %copy-start.6 = (f32[1,1,256,512]{3,2,1,0:T(8,128)S(1)}, f32[1,1,256,512]{3,2,1,0:T(8,128)}, u32[]{:S(2)}) copy-start(f32[1,1,256,512]{3,2,1,0:T(8,128)} %param.6) | copy-start | bytes 1572868
  0.6 7.3 %copy-start.5 = (f32[1,1,256,512]{3,2,1,0:T(8,128)S(1)}, f32[1,1,256,512]{3,2,1,0:T(8,128)}, u32[]{:S(2)}) copy-start(f32[1,1,256,512]{3,2,1,0:T(8,128)} %param.5) | copy-start | bytes 1572868
  13.0 29.9 %all-to-all-start.1 = ((f32[1,1,256,512]{2,1,0,3:T(1,128)}), f32[1,1,256,512]{2,1,0,3:T(1,128)S(1)}, u32[]{:S(2)}, u32[]{:S(2)}) async-start(f32[1,1,256,512]{2,1,0,3:T(1,128)} %copy.10), calls=%async_computation.1 | async-start | bytes 1048576 | tf_op jit(solution)/shard_map/all_to_all | solution.py:49
  42.9 10.9 %copy-start.2 = (f32[1,1,256,512]{2,1,0,3:T(1,128)}, f32[1,1,256,512]{2,1,0,3:T(1,128)S(1)}, u32[]{:S(2)}) copy-start(f32[1,1,256,512]{2,1,0,3:T(1,128)S(1)} %all-to-all-done.1) | copy-start | bytes 1572868
  42.9 22.0 %all-to-all-start = ((f32[1,1,256,512]{2,1,0,3:T(1,128)}), f32[1,1,256,512]{2,1,0,3:T(1,128)}, u32[]{:S(2)}, u32[]{:S(2)}) async-start(f32[1,1,256,512]{2,1,0,3:T(1,128)} %copy.8), calls=%async_computation | async-start | bytes 1048576 | tf_op jit(solution)/shard_map/all_to_all | solution.py:48
  72.0 19.8 %all-to-all-start.3 = ((f32[1,1,256,512]{2,1,0,3:T(1,128)}), f32[1,1,256,512]{2,1,0,3:T(1,128)S(1)}, u32[]{:S(2)}, u32[]{:S(2)}) async-start(f32[1,1,256,512]{2,1,0,3:T(1,128)} %copy.12), calls=%async_computation.3 | async-start | bytes 1048576 | tf_op jit(solution)/shard_map/all_to_all | solution.py:57
  91.8 5.1 %copy-start.3 = (f32[1,1,256,512]{2,1,0,3:T(1,128)}, f32[1,1,256,512]{2,1,0,3:T(1,128)S(1)}, u32[]{:S(2)}) copy-start(f32[1,1,256,512]{2,1,0,3:T(1,128)S(1)} %all-to-all-done.3) | copy-start | bytes 1572868
  91.8 18.8 %all-to-all-start.2 = ((f32[1,1,256,512]{2,1,0,3:T(1,128)}), f32[1,1,256,512]{2,1,0,3:T(1,128)}, u32[]{:S(2)}, u32[]{:S(2)}) async-start(f32[1,1,256,512]{2,1,0,3:T(1,128)} %copy.11), calls=%async_computation.2 | async-start | bytes 1048576 | tf_op jit(solution)/shard_map/all_to_all | solution.py:56
  96.9 4.7 %copy-start.4 = (f32[1,1,256,512]{2,1,0,3:T(1,128)S(1)}, f32[1,1,256,512]{2,1,0,3:T(1,128)}, u32[]{:S(2)}) copy-start(f32[1,1,256,512]{2,1,0,3:T(1,128)} %copy-done.3) | copy-start | bytes 1572868
  117.8 25.1 %all-to-all-start.5 = ((f32[1,1,256,512]{2,1,0,3:T(1,128)}), f32[1,1,256,512]{2,1,0,3:T(1,128)S(1)}, u32[]{:S(2)}, u32[]{:S(2)}) async-start(f32[1,1,256,512]{2,1,0,3:T(1,128)} %copy.14), calls=%async_computation.5 | async-start | bytes 1048576 | tf_op jit(solution)/shard_map/all_to_all | solution.py:49
  142.9 5.2 %copy-start = (f32[1,1,256,512]{2,1,0,3:T(1,128)}, f32[1,1,256,512]{2,1,0,3:T(1,128)S(1)}, u32[]{:S(2)}) copy-start(f32[1,1,256,512]{2,1,0,3:T(1,128)S(1)} %all-to-all-done.5) | copy-start | bytes 1572868
  142.9 21.2 %all-to-all-start.4 = ((f32[1,1,256,512]{2,1,0,3:T(1,128)}), f32[1,1,256,512]{2,1,0,3:T(1,128)}, u32[]{:S(2)}, u32[]{:S(2)}) async-start(f32[1,1,256,512]{2,1,0,3:T(1,128)} %copy.13), calls=%async_computation.4 | async-start | bytes 1048576 | tf_op jit(solution)/shard_map/all_to_all | solution.py:48
  148.1 4.7 %copy-start.1 = (f32[1,1,256,512]{2,1,0,3:T(1,128)S(1)}, f32[1,1,256,512]{2,1,0,3:T(1,128)}, u32[]{:S(2)}) copy-start(f32[1,1,256,512]{2,1,0,3:T(1,128)} %copy-done) | copy-start | bytes 1572868
where the time goes:
time: 171 us; the launch traced here: 170 us
  waiting for transfers between devices  78 us (46%)
  matrix products  42.7 us (25%)
  starting transfers between devices  37.9 us (22%)
  local copies, waits for them, and re-layouts  9.5 us (6%)
    all_to_all x2, waiting for transfers between devices, inner_step(): lax.all_to_all(plane_imag, 'inner', split_axis=3, concat_axis=3, tiled=True)  36 us
    all_to_all x2, waiting for transfers between devices, inner_step(): lax.all_to_all(plane_real, 'inner', split_axis=3, concat_axis=3, tiled=True)  21.2 us
    all_to_all x2, starting transfers between devices, inner_step(): lax.all_to_all(plane_imag, 'inner', split_axis=3, concat_axis=3, tiled=True)  16.5 us
    all_to_all x1, waiting for transfers between devices, outer_step(): lax.all_to_all(plane_imag, 'outer', split_axis=3, concat_axis=3, tiled=True)  12.9 us
    dot_general x4, matrix products, product(): jnp.dot(left_real + left_imag, moved_sum, precision=lax.Precision.HIGHEST...  11 us
    all_to_all x2, starting transfers between devices, inner_step(): lax.all_to_all(plane_real, 'inner', split_axis=3, concat_axis=3, tiled=True)  10.5 us
    dot_general x4, matrix products, prepare(): jnp.dot(selector, branch_imag, precision=lax.Precision.HIGHEST, preferred...  9.35 us
    dot_general x4, matrix products, prepare(): jnp.dot(selector, branch_real, precision=lax.Precision.HIGHEST, preferred...  9.24 us
  transfers between devices with their start and end apart: 6, of which 6 were waited for; matrix products, arithmetic and copies ran while one was open for 12% of the time, Pallas kernels for 0%

commit v1 on v0

--- a/solution.py
+++ b/solution.py
@@ -45,7 +45,12 @@
 
 def inner_step(plane_real, plane_imag, prepared):
     return product(
-        lax.all_to_all(plane_real, "inner", split_axis=3, concat_axis=3, tiled=True),
+        jnp.concatenate(
+            lax.all_to_all(
+                jnp.stack(jnp.split(plane_real, lax.axis_size("inner"), axis=3)), "inner", 0, 0
+            ),
+            axis=3,
+        ),
         lax.all_to_all(plane_imag, "inner", split_axis=3, concat_axis=3, tiled=True),
         prepared,
     )

time: 171 us -> 217 us (1.27)
  local copies, waits for them, and re-layouts: 9.5 us -> 60.5 us
  waiting for transfers between devices: 78 us -> 69.4 us
    unnamed x14 -> x36, local copies, waits for them, and re-layouts: 0.03 us -> 29.1 us
    another operation x0 -> x19, local copies, waits for them, and re-layouts: none -> 24.3 us  [inner_step(): jnp.stack(jnp.split(plane_real, lax.axis_size('inner'), axis=3))]
    all_to_all x2, waiting for transfers between devices: 36 us -> 19.3 us  [inner_step(): lax.all_to_all(plane_imag, 'inner', split_axis=3, concat_axis=3, tiled=True)]
    all_to_all x2, waiting for transfers between devices: 21.2 us -> 29.2 us  [inner_step(): lax.all_to_all(jnp.stack(jnp.split(plane_real, lax.axis_size('inner'), ax...]
    all_to_all x2, starting transfers between devices: 10.5 us -> 17.1 us  [inner_step(): lax.all_to_all(jnp.stack(jnp.split(plane_real, lax.axis_size('inner'), ax...]
    all_to_all x2, starting transfers between devices: 16.5 us -> 9.86 us  [inner_step(): lax.all_to_all(plane_imag, 'inner', split_axis=3, concat_axis=3, tiled=True)]
    reshape x3 -> x1, local copies, waits for them, and re-layouts: 3.41 us -> 1.04 us  [product(): (first - second).reshape(1, 1, count, width)]
  transfers between devices with their start and end apart: 6 -> 6, of which waited for: 6 -> 6; matrix products, arithmetic and copies ran while one was open for 12% -> 14% of each run, Pallas kernels for 0% -> 0%
where the time goes in v1:
time: 217 us; the launch traced here: 215 us
  waiting for transfers between devices  69.4 us (32%)
  local copies, waits for them, and re-layouts  60.5 us (28%)
  matrix products  44.8 us (21%)
  starting transfers between devices  37.9 us (17%)
    all_to_all x2, waiting for transfers between devices, inner_step(): lax.all_to_all(jnp.stack(jnp.split(plane_real, lax.axis_size('inner'), ax...  29.2 us
    unnamed x36, local copies, waits for them, and re-layouts  29.1 us
    another operation x19, local copies, waits for them, and re-layouts, inner_step(): jnp.stack(jnp.split(plane_real, lax.axis_size('inner'), axis=3))  24.3 us
    all_to_all x2, waiting for transfers between devices, inner_step(): lax.all_to_all(plane_imag, 'inner', split_axis=3, concat_axis=3, tiled=True)  19.3 us
    all_to_all x2, starting transfers between devices, inner_step(): lax.all_to_all(jnp.stack(jnp.split(plane_real, lax.axis_size('inner'), ax...  17.1 us
    all_to_all x1, waiting for transfers between devices, outer_step(): lax.all_to_all(plane_imag, 'outer', split_axis=3, concat_axis=3, tiled=True)  12.9 us
    dot_general x4, matrix products, product(): jnp.dot(left_real + left_imag, moved_sum, precision=lax.Precision.HIGHEST...  12.2 us
    all_to_all x2, starting transfers between devices, inner_step(): lax.all_to_all(plane_imag, 'inner', split_axis=3, concat_axis=3, tiled=True)  9.86 us
  transfers between devices with their start and end apart: 6, of which 6 were waited for; matrix products, arithmetic and copies ran while one was open for 14% of the time, Pallas kernels for 0%

profile of v1, /device:TPU:33, one launch (start us, length us, event | category | flops | bytes accessed | tf_op | source)
XLA Modules:
  0.0 214.6 jit_solution(7736206687082433146)
XLA Ops:
  1.5 2.3 %fusion.20 = f32[512,512]{1,0:T(8,128)S(1)} fusion(f32[4,512,512]{2,1,0:T(8,128)} %param.8, s32[512]{0:T(512)S(1)} %bitcast.202), kind=kOutput, calls=%fused_computation.26 | convolution fusion | flops 1610874880 | bytes 2099200 | tf_op jit(solution)/shard_map/dot_general | solution.py:16
  3.8 2.3 %fusion.22 = f32[512,512]{1,0:T(8,128)S(1)} fusion(f32[4,512,512]{2,1,0:T(8,128)} %param.7, s32[512]{0:T(512)S(1)} %bitcast.203), kind=kOutput, calls=%fused_computation.28 | convolution fusion | flops 1610874880 | bytes 2099200 | tf_op jit(solution)/shard_map/dot_general | solution.py:13
  19.7 10.7 %all-to-all-start = ((f32[16,1,1,256,32]{3,4,2,1,0:T(8,128)}), f32[16,1,1,256,32]{3,4,2,1,0:T(8,128)}, u32[]{:S(2)}, u32[]{:S(2)}) async-start(f32[16,1,1,256,32]{3,4,2,1,0:T(8,128)} %constant_dynamic-update-slice_fusion), calls=%async_computation | async-start | bytes 1048576 | tf_op jit(solution)/shard_map/all_to_all | solution.py:49
  30.5 3.0 %fusion.1 = f32[1,1,256,512]{2,3,1,0:T(8,128)S(1)} fusion(f32[256,512]{0,1:T(8,128)S(1)} %convolution_bitcast_fusion, f32[256,512]{0,1:T(8,128)S(1)} %convolution_bitcast_fusion.1, f32[512,512]{1,0:T(8,128)S(1)} %fusion.22, f32[512,512]{1,0:T(8,128)S(1)} %fusion.20, f32[1,1,256,512]{3,2,1,0:T(8,128)} %param.6, f32[1,1,256,512]{3,2,1,0:T(8,128)} %param.5), kind=kOutput, calls=%fused_computation.5 | convolution fusion | flops 805961728 | bytes 4718592 | tf_op jit(solution)/shard_map/dot_general | solution.py:34
  34.8 14.9 %all-to-all-done = f32[16,1,1,256,32]{3,4,2,1,0:T(8,128)} async-done(((f32[16,1,1,256,32]{3,4,2,1,0:T(8,128)}), f32[16,1,1,256,32]{3,4,2,1,0:T(8,128)}, u32[]{:S(2)}, u32[]{:S(2)}) %all-to-all-start) | async-done | bytes 524320 | tf_op jit(solution)/shard_map/all_to_all | solution.py:49
  49.8 5.2 %all-to-all-start.1 = ((f32[1,1,256,512]{2,1,0,3:T(1,128)}), f32[1,1,256,512]{2,1,0,3:T(1,128)}, u32[]{:S(2)}, u32[]{:S(2)}) async-start(f32[1,1,256,512]{2,1,0,3:T(1,128)} %copy.13), calls=%async_computation.1 | async-start | bytes 1048576 | tf_op jit(solution)/shard_map/all_to_all | solution.py:54
  55.0 2.3 %fusion.18 = f32[512,512]{1,0:T(8,128)S(1)} fusion(f32[4,512,512]{2,1,0:T(8,128)} %param.7, s32[512]{0:T(512)S(1)} %bitcast.200), kind=kOutput, calls=%fused_computation.24 | convolution fusion | flops 1610874880 | bytes 2099200 | tf_op jit(solution)/shard_map/dot_general | solution.py:13
  57.3 2.3 %fusion.16 = f32[512,512]{1,0:T(8,128)S(1)} fusion(f32[4,512,512]{2,1,0:T(8,128)} %param.8, s32[512]{0:T(512)S(1)} %bitcast.201), kind=kOutput, calls=%fused_computation.22 | convolution fusion | flops 1610874880 | bytes 2099200 | tf_op jit(solution)/shard_map/dot_general | solution.py:16
  61.7 10.0 %all-to-all-done.1 = f32[1,1,256,512]{2,1,0,3:T(1,128)} async-done(((f32[1,1,256,512]{2,1,0,3:T(1,128)}), f32[1,1,256,512]{2,1,0,3:T(1,128)}, u32[]{:S(2)}, u32[]{:S(2)}) %all-to-all-start.1) | async-done | bytes 524320 | tf_op jit(solution)/shard_map/all_to_all | solution.py:54
  73.8 3.1 %fusion.3 = f32[1,1,256,512]{3,2,1,0:T(8,128)} fusion(f32[256,512]{1,0:T(8,128)S(1)} %fusion.43, f32[256,512]{1,0:T(8,128)S(1)} %fusion.65, f32[512,512]{1,0:T(8,128)S(1)} %fusion.18, f32[512,512]{1,0:T(8,128)S(1)} %fusion.16, f32[256,512]{0,1:T(8,128)} %bitcast.25, f32[1,1,256,512]{2,1,0,3:T(1,128)} %all-to-all-done.1), kind=kOutput, calls=%fused_computation.7 | convolution fusion | flops 805961728 | bytes 4718592 | tf_op jit(solution)/shard_map/dot_general | solution.py:34
  78.9 5.8 %all-to-all-start.3 = ((f32[1,1,256,512]{2,1,0,3:T(1,128)}), f32[1,1,256,512]{2,1,0,3:T(1,128)S(1)}, u32[]{:S(2)}, u32[]{:S(2)}) async-start(f32[1,1,256,512]{2,1,0,3:T(1,128)} %copy.15), calls=%async_computation.3 | async-start | bytes 1048576 | tf_op jit(solution)/shard_map/all_to_all | solution.py:62
  85.8 12.9 %all-to-all-done.3 = f32[1,1,256,512]{2,1,0,3:T(1,128)S(1)} async-done(((f32[1,1,256,512]{2,1,0,3:T(1,128)}), f32[1,1,256,512]{2,1,0,3:T(1,128)S(1)}, u32[]{:S(2)}, u32[]{:S(2)}) %all-to-all-start.3) | async-done | bytes 524320 | tf_op jit(solution)/shard_map/all_to_all | solution.py:62
  98.7 5.1 %all-to-all-start.2 = ((f32[1,1,256,512]{2,1,0,3:T(1,128)}), f32[1,1,256,512]{2,1,0,3:T(1,128)}, u32[]{:S(2)}, u32[]{:S(2)}) async-start(f32[1,1,256,512]{2,1,0,3:T(1,128)} %copy.14), calls=%async_computation.2 | async-start | bytes 1048576 | tf_op jit(solution)/shard_map/all_to_all | solution.py:61
  103.8 2.3 %fusion.12 = f32[512,512]{1,0:T(8,128)S(1)} fusion(f32[4,512,512]{2,1,0:T(8,128)} %param.8, s32[512]{0:T(512)S(1)} %bitcast.198), kind=kOutput, calls=%fused_computation.18 | convolution fusion | flops 1610874880 | bytes 2099200 | tf_op jit(solution)/shard_map/dot_general | solution.py:16
  106.1 2.3 %fusion.14 = f32[512,512]{1,0:T(8,128)S(1)} fusion(f32[4,512,512]{2,1,0:T(8,128)} %param.7, s32[512]{0:T(512)S(1)} %bitcast.199), kind=kOutput, calls=%fused_computation.20 | convolution fusion | flops 1610874880 | bytes 2099200 | tf_op jit(solution)/shard_map/dot_general | solution.py:13
  109.5 8.0 %all-to-all-done.2 = f32[1,1,256,512]{2,1,0,3:T(1,128)} async-done(((f32[1,1,256,512]{2,1,0,3:T(1,128)}), f32[1,1,256,512]{2,1,0,3:T(1,128)}, u32[]{:S(2)}, u32[]{:S(2)}) %all-to-all-start.2) | async-done | bytes 524320 | tf_op jit(solution)/shard_map/all_to_all | solution.py:61
  163.3 6.4 %all-to-all-start.4 = ((f32[16,1,1,256,32]{3,4,2,1,0:T(8,128)}), f32[16,1,1,256,32]{3,4,2,1,0:T(8,128)}, u32[]{:S(2)}, u32[]{:S(2)}) async-start(f32[16,1,1,256,32]{3,4,2,1,0:T(8,128)} %constant_dynamic-update-slice_fusion.16), calls=%async_computation.4 | async-start | bytes 1048576 | tf_op jit(solution)/shard_map/all_to_all | solution.py:49
  169.7 3.1 %fusion.5 = f32[1,1,256,512]{3,2,1,0:T(8,128)} fusion(f32[256,512]{1,0:T(8,128)S(1)} %fusion.38, f32[256,512]{1,0:T(8,128)S(1)} %fusion.41, f32[512,512]{1,0:T(8,128)S(1)} %fusion.14, f32[512,512]{1,0:T(8,128)S(1)} %fusion.12, f32[1,1,256,512]{2,1,0,3:T(1,128)} %copy-done, f32[1,1,256,512]{2,1,0,3:T(1,128)} %all-to-all-done.2), kind=kOutput, calls=%fused_computation.9 | convolution fusion | flops 805961728 | bytes 4718592 | tf_op jit(solution)/shard_map/dot_general | solution.py:34
  174.8 14.3 %all-to-all-done.4 = f32[16,1,1,256,32]{3,4,2,1,0:T(8,128)} async-done(((f32[16,1,1,256,32]{3,4,2,1,0:T(8,128)}), f32[16,1,1,256,32]{3,4,2,1,0:T(8,128)}, u32[]{:S(2)}, u32[]{:S(2)}) %all-to-all-start.4) | async-done | bytes 524320 | tf_op jit(solution)/shard_map/all_to_all | solution.py:49
  189.1 4.6 %all-to-all-start.5 = ((f32[1,1,256,512]{2,1,0,3:T(1,128)}), f32[1,1,256,512]{2,1,0,3:T(1,128)S(1)}, u32[]{:S(2)}, u32[]{:S(2)}) async-start(f32[1,1,256,512]{2,1,0,3:T(1,128)} %copy.33), calls=%async_computation.5 | async-start | bytes 1048576 | tf_op jit(solution)/shard_map/all_to_all | solution.py:54
  193.7 2.3 %fusion.8 = f32[512,512]{1,0:T(8,128)S(1)} fusion(f32[4,512,512]{2,1,0:T(8,128)} %param.8, s32[512]{0:T(512)S(1)} %bitcast.196), kind=kOutput, calls=%fused_computation.14 | convolution fusion | flops 1610874880 | bytes 2099200 | tf_op jit(solution)/shard_map/dot_general | solution.py:16
  196.0 2.3 %fusion.10 = f32[512,512]{1,0:T(8,128)S(1)} fusion(f32[4,512,512]{2,1,0:T(8,128)} %param.7, s32[512]{0:T(512)S(1)} %bitcast.197), kind=kOutput, calls=%fused_computation.16 | convolution fusion | flops 1610874880 | bytes 2099200 | tf_op jit(solution)/shard_map/dot_general | solution.py:13
  200.4 9.3 %all-to-all-done.5 = f32[1,1,256,512]{2,1,0,3:T(1,128)S(1)} async-done(((f32[1,1,256,512]{2,1,0,3:T(1,128)}), f32[1,1,256,512]{2,1,0,3:T(1,128)S(1)}, u32[]{:S(2)}, u32[]{:S(2)}) %all-to-all-start.5) | async-done | bytes 524320 | tf_op jit(solution)/shard_map/all_to_all | solution.py:54
  211.7 3.0 %fusion.7 = f32[1,1,256,512]{3,2,1,0:T(8,128)} fusion(f32[256,512]{1,0:T(8,128)S(1)} %fusion.36, f32[256,512]{1,0:T(8,128)S(1)} %fusion.66, f32[512,512]{1,0:T(8,128)S(1)} %fusion.10, f32[512,512]{1,0:T(8,128)S(1)} %fusion.8, f32[256,512]{0,1:T(8,128)} %bitcast.55, f32[1,1,256,512]{2,1,0,3:T(1,128)S(1)} %all-to-all-done.5), kind=kOutput, calls=%fused_computation.11 | convolution fusion | flops 805961728 | bytes 4718592 | tf_op jit(solution)/shard_map/dot_general | solution.py:34
  (72 shorter events, 75.8 us)
Async XLA Ops:
  0.6 5.5 %copy-start.2 = (f32[1,1,256,512]{3,2,1,0:T(8,128)S(1)}, f32[1,1,256,512]{3,2,1,0:T(8,128)}, u32[]{:S(2)}) copy-start(f32[1,1,256,512]{3,2,1,0:T(8,128)} %param.6) | copy-start | bytes 1572868
  0.6 7.3 %copy-start.1 = (f32[1,1,256,512]{3,2,1,0:T(8,128)S(1)}, f32[1,1,256,512]{3,2,1,0:T(8,128)}, u32[]{:S(2)}) copy-start(f32[1,1,256,512]{3,2,1,0:T(8,128)} %param.5) | copy-start | bytes 1572868
  19.7 30.0 %all-to-all-start = ((f32[16,1,1,256,32]{3,4,2,1,0:T(8,128)}), f32[16,1,1,256,32]{3,4,2,1,0:T(8,128)}, u32[]{:S(2)}, u32[]{:S(2)}) async-start(f32[16,1,1,256,32]{3,4,2,1,0:T(8,128)} %constant_dynamic-update-slice_fusion), calls=%async_computation | async-start | bytes 1048576 | tf_op jit(solution)/shard_map/all_to_all | solution.py:49
  49.8 22.0 %all-to-all-start.1 = ((f32[1,1,256,512]{2,1,0,3:T(1,128)}), f32[1,1,256,512]{2,1,0,3:T(1,128)}, u32[]{:S(2)}, u32[]{:S(2)}) async-start(f32[1,1,256,512]{2,1,0,3:T(1,128)} %copy.13), calls=%async_computation.1 | async-start | bytes 1048576 | tf_op jit(solution)/shard_map/all_to_all | solution.py:54
  78.9 19.8 %all-to-all-start.3 = ((f32[1,1,256,512]{2,1,0,3:T(1,128)}), f32[1,1,256,512]{2,1,0,3:T(1,128)S(1)}, u32[]{:S(2)}, u32[]{:S(2)}) async-start(f32[1,1,256,512]{2,1,0,3:T(1,128)} %copy.15), calls=%async_computation.3 | async-start | bytes 1048576 | tf_op jit(solution)/shard_map/all_to_all | solution.py:62
  98.7 10.8 %copy-start = (f32[1,1,256,512]{2,1,0,3:T(1,128)}, f32[1,1,256,512]{2,1,0,3:T(1,128)S(1)}, u32[]{:S(2)}) copy-start(f32[1,1,256,512]{2,1,0,3:T(1,128)S(1)} %all-to-all-done.3) | copy-start | bytes 1572868
  98.7 18.8 %all-to-all-start.2 = ((f32[1,1,256,512]{2,1,0,3:T(1,128)}), f32[1,1,256,512]{2,1,0,3:T(1,128)}, u32[]{:S(2)}, u32[]{:S(2)}) async-start(f32[1,1,256,512]{2,1,0,3:T(1,128)} %copy.14), calls=%async_computation.2 | async-start | bytes 1048576 | tf_op jit(solution)/shard_map/all_to_all | solution.py:61
  163.3 25.8 %all-to-all-start.4 = ((f32[16,1,1,256,32]{3,4,2,1,0:T(8,128)}), f32[16,1,1,256,32]{3,4,2,1,0:T(8,128)}, u32[]{:S(2)}, u32[]{:S(2)}) async-start(f32[16,1,1,256,32]{3,4,2,1,0:T(8,128)} %constant_dynamic-update-slice_fusion.16), calls=%async_computation.4 | async-start | bytes 1048576 | tf_op jit(solution)/shard_map/all_to_all | solution.py:49
  189.1 20.7 %all-to-all-start.5 = ((f32[1,1,256,512]{2,1,0,3:T(1,128)}), f32[1,1,256,512]{2,1,0,3:T(1,128)S(1)}, u32[]{:S(2)}, u32[]{:S(2)}) async-start(f32[1,1,256,512]{2,1,0,3:T(1,128)} %copy.33), calls=%async_computation.5 | async-start | bytes 1048576 | tf_op jit(solution)/shard_map/all_to_all | solution.py:54
